TPU v7x, 32 devices: a whole 2x2x4 slice. The times are simulated.
32 devices in a mesh: blk: 8 (over y, x, core), chan: 4 (over z).
Axes of the slice: x: 2, y: 2, z: 4, core: 2. Of those that a mesh axis runs over, the one named last changes fastest.
Arguments:
- pair_repr: bfloat16 [512, 512, 128], P('blk', 'chan'), may hold values from -6 to 6
- chain_lengths: int32 [8], replicated, may hold values from 48 to 64
- norm_gain: float32 [128], replicated, may hold values from 0.1 to 1.9
- norm_bias: float32 [128], replicated, may hold values from -3 to 3
- left_gate: bfloat16 [128, 128], replicated, may hold values from -0.5 to 0.5
- left_value: bfloat16 [128, 128], replicated, may hold values from -0.5 to 0.5
- right_gate: bfloat16 [128, 128], replicated, may hold values from -0.5 to 0.5
- right_value: bfloat16 [128, 128], replicated, may hold values from -0.5 to 0.5
- out_gain: float32 [128], replicated, may hold values from 0.1 to 1.9
- out_bias: float32 [128], replicated, may hold values from -3 to 3
- out_weight: bfloat16 [128, 128], replicated, may hold values from -0.5 to 0.5
- gate_weight: bfloat16 [128, 128], replicated, may hold values from -0.5 to 0.5
Outputs:
- pair_update: bfloat16 [512, 104, 128], P('blk', 'chan')
Inputs may be any that keep to these rules, and one draw needn't show every extreme that they name: Chain slot s covers residues s * 64 to (s + 1) * 64 - 1, of which the first chain_lengths[s] are real and the rest padding.
All inputs are finite; a program needn't handle non-finite values.
Results may differ from a plain program's by a relative error of at most 0.0058.
Values may be sent and summed in bfloat16 or wider, within the bound.
A program may use at most 64 MiB of HBM per device.

v0:
```python
import functools

import jax
import jax.numpy as jnp
from jax import lax
from jax.experimental import pallas as pl
from jax.experimental.pallas import tpu as pltpu
from jax.sharding import PartitionSpec as P

JD = 13
PAD = 16
EPS = 1e-05
F32 = jnp.float32
BF16 = jnp.bfloat16
NT = (((1,), (1,)), ((), ()))
TN = (((0,), (0,)), ((), ()))
NN = (((1,), (0,)), ((), ()))


def xor(a, b, n):
    total, bit = 0, 1
    while bit < n:
        total = total + bit * ((a // bit + b // bit) % 2)
        bit *= 2
    return total


def reverse_bits(t, n):
    total, bit = 0, 1
    while bit < n:
        total = total + (n // 2 // bit) * ((t // bit) % 2)
        bit *= 2
    return total


def sigmoid(x):
    return 0.5 * jnp.tanh(0.5 * x) + 0.5


def layer_norm(x, gain, bias):
    centre = jnp.mean(x, axis=-1, keepdims=True)
    centred = x - centre
    spread = jnp.mean(centred * centred, axis=-1, keepdims=True)
    return centred * lax.rsqrt(spread + EPS) * gain + bias


def kernel(
    n_pos,
    slot_size,
    lens,
    pair_hbm,
    gain,
    bias,
    lgate,
    lvalue,
    rgate,
    rvalue,
    ogain,
    obias,
    oweight,
    gweight,
    out,
    pair,
    weights,
    right_all,
    left,
    r0,
    r1,
    work,
    send,
    own,
    recv,
    gate_in,
    gate_val,
    update,
    load_sem,
    rs_send,
    rs_recv,
    fw_send,
    fw_recv,
    ps_send,
    ps_recv,
    relay,
    rl_send,
    rl_recv,
):
    rows, cols, ch = pair.shape
    hid = lgate.shape[1]
    blk = lax.axis_index("blk")
    z = lax.axis_index("chan")
    q = blk // 2
    h = blk % 2
    partner = 2 * q + 1 - h

    load_a = pltpu.make_async_copy(
        pair_hbm.at[pl.ds(0, JD)], pair.at[pl.ds(0, JD)], load_sem.at[0]
    )
    load_b = pltpu.make_async_copy(
        pair_hbm.at[pl.ds(JD, rows - JD)], pair.at[pl.ds(JD, rows - JD)], load_sem.at[1]
    )
    load_a.start()
    load_b.start()

    barrier = pltpu.get_barrier_semaphore()
    for d in range(1, n_pos):
        pl.semaphore_signal(barrier, inc=1, device_id={"blk": 2 * xor(q, d, n_pos) + h})
        pl.semaphore_signal(barrier, inc=1, device_id={"chan": xor(z, d, n_pos)})
    pl.semaphore_signal(barrier, inc=1, device_id={"blk": partner})

    for n, w in enumerate((rgate, rvalue, lgate, lvalue)):
        weights[n * hid : (n + 1) * hid, :] = w[...].astype(F32).T.astype(BF16)

    col = z * cols + lax.broadcasted_iota(jnp.int32, (1, cols), 1)
    chain = col // slot_size
    chain_len = jnp.zeros_like(col)
    for s in range(lens.shape[0]):
        chain_len = jnp.where(chain == s, lens[s], chain_len)
    col_real = (col % slot_size < chain_len).astype(F32)

    def row_real(i):
        pos = blk * rows + i
        return jnp.where(pos % slot_size < lens[pos // slot_size], 1.0, 0.0).astype(F32)

    gain_v, bias_v = gain[...], bias[...]

    def norm_rows(i, count):
        x = pair[pl.ds(i, count)].astype(F32).reshape(count * cols, ch)
        return layer_norm(x, gain_v, bias_v).astype(BF16)

    load_a.wait()

    def right_row(m, carry):
        normed = norm_rows(m, 1)
        mix = lax.dot_general(weights[: 2 * hid, :], normed, NT, preferred_element_type=F32)
        val = sigmoid(mix[:hid]) * mix[hid:] * (col_real * row_real(m))
        right_all[blk, pl.ds(pl.multiple_of(m * hid, hid), hid), :] = val.astype(BF16)
        return carry

    for m in range(JD):
        right_row(m, 0)

    pl.semaphore_wait(barrier, 2 * (n_pos - 1) + 1)

    def right_copy(d):
        return pltpu.make_async_remote_copy(
            src_ref=right_all.at[blk],
            dst_ref=right_all.at[blk],
            send_sem=rs_send.at[d],
            recv_sem=rs_recv.at[d],
            device_id={"blk": 2 * xor(q, d, n_pos) + h},
        )

    def forward_copy(d):
        mine = 2 * xor(q, d, n_pos) + h
        return pltpu.make_async_remote_copy(
            src_ref=right_all.at[mine],
            dst_ref=right_all.at[mine],
            send_sem=fw_send.at[d],
            recv_sem=fw_recv.at[d],
            device_id={"blk": partner},
        )

    forward_copy(0).start()
    for t in range(1, n_pos):
        right_copy(reverse_bits(t, n_pos)).start()

    load_b.wait()

    def left_rows(t, carry):
        i = 8 * t
        normed = norm_rows(i, 8)
        for u in range(8):
            for g in range(2):
                at = pl.ds(pl.multiple_of((i + u) * 2 * PAD, 2 * PAD) + g * JD, JD)
                gate_in[at, :] = normed[
                    u * cols + g * rows : u * cols + g * rows + JD
                ].astype(F32)
        mix = lax.dot_general(weights[2 * hid :, :], normed, NT, preferred_element_type=F32)
        val = sigmoid(mix[:hid]) * mix[hid:]
        for u in range(8):
            left[pl.ds(i + u, hid, stride=rows + 8), :] = val[:, u * cols : (u + 1) * cols] * (
                col_real * row_real(i + u)
            )
        return carry

    lax.fori_loop(0, rows // 8, left_rows, 0)

    def partial_copy(p):
        e = xor(z, p, n_pos)
        return pltpu.make_async_remote_copy(
            src_ref=send.at[p],
            dst_ref=recv.at[e],
            send_sem=ps_send.at[e],
            recv_sem=ps_recv.at[e],
            device_id={"chan": p},
        )

    wide = 8 * 2 * PAD

    def gates(g, carry):
        at = pl.ds(pl.multiple_of(g * wide, wide), wide)
        mix = lax.dot_general(
            gate_in[at, :].astype(BF16), gweight[...], NN, preferred_element_type=F32
        )
        gate_val[at, :] = sigmoid(mix)
        return carry

    last = n_pos - 1
    half = n_pos // 2

    def relayed(source, p):
        ends = ((source == 0) & (p >= half)) | ((source == last) & (p < half))
        return ends & ((p + q) % 2 == 1)

    next_in = jnp.where(z == 0, 1, jnp.where(z == last, last - 1, -1))
    behind = jnp.where(z == 1, 0, jnp.where(z == last - 1, last, -1))

    def relay_copy(p):
        return pltpu.make_async_remote_copy(
            src_ref=send.at[p],
            dst_ref=relay.at[p],
            send_sem=rl_send.at[p],
            recv_sem=rl_recv.at[p],
            device_id={"chan": jnp.where(z < half, 1, last - 1)},
        )

    def stage(t, carry):
        d = reverse_bits(t, n_pos)
        p = xor(q, d, n_pos)

        @pl.when(d > 0)
        def _():
            right_copy(d).wait_recv()
            forward_copy(d).start()

        forward_copy(d).wait_recv()
        for g, dst in enumerate((r0, r1)):
            for m in range(JD):
                dst[pl.ds(m, hid, stride=PAD + 8), :] = right_all[
                    2 * p + g, m * hid : (m + 1) * hid, :
                ].astype(F32)

        def channels(t, inner):
            for u in range(32):
                c = 32 * t + u
                rr = pl.ds(pl.multiple_of(c * (PAD + 8), 8), PAD)
                lhs = jnp.concatenate([r0[rr, :], r1[rr, :]], axis=0).astype(BF16)
                lc = left[pl.ds(pl.multiple_of(c * (rows + 8), 8), rows), :].astype(BF16)
                o = lax.dot_general(lhs, lc, NT, preferred_element_type=F32)
                work[pl.ds(c, PAD, stride=hid + 8), :] = jnp.concatenate([o[:PAD], o[PAD:]], axis=1)
            return inner

        lax.fori_loop(0, hid // 32, channels, 0)
        @pl.when(p == z)
        def _():
            for m in range(JD):
                own[m * hid : (m + 1) * hid, :] = work[m * (hid + 8) : m * (hid + 8) + hid, :]

        @pl.when(p != z)
        def _():
            for m in range(JD):
                send[p, m * hid : (m + 1) * hid, :] = work[
                    m * (hid + 8) : m * (hid + 8) + hid, :
                ].astype(BF16)

            @pl.when(relayed(z, p))
            def _():
                relay_copy(p).start()

            later = (p == next_in) | relayed(behind, p)

            @pl.when(jnp.logical_not(relayed(z, p) | later))
            def _():
                partial_copy(p).start()

        return carry

    lax.fori_loop(0, n_pos, stage, 0)

    @pl.when(next_in >= 0)
    def _():
        partial_copy(next_in).start()

    def pass_on(t, carry):
        p = xor(q, reverse_bits(half + t, n_pos), n_pos)

        @pl.when(relayed(behind, p))
        def _():
            relay_copy(p).wait_recv()
            for m in range(JD):
                here = slice(m * hid, (m + 1) * hid)
                send[p, here, :] = (
                    send[p, here, :].astype(F32) + relay[p, here, :].astype(F32)
                ).astype(BF16)
            partial_copy(p).start()

        return carry

    lax.fori_loop(0, rows // 8, gates, 0)
    lax.fori_loop(0, half, pass_on, 0)

    ogain_v = jnp.broadcast_to(ogain[...], (2 * rows, hid)).T
    obias_v = jnp.broadcast_to(obias[...], (2 * rows, hid)).T
    for e in range(1, n_pos):
        source = xor(z, e, n_pos)

        @pl.when(jnp.logical_not(relayed(source, z)))
        def _():
            partial_copy(source).wait_recv()

    def finish(m):
        here = slice(m * hid, (m + 1) * hid)
        total = own[here, :]
        for e in range(1, n_pos):
            more = recv[e, here, :].astype(F32)
            total = total + jnp.where(relayed(xor(z, e, n_pos), z), 0.0, more)
        total = total.astype(BF16).astype(F32)
        centred = total - jnp.mean(total, axis=0, keepdims=True)
        spread = jnp.mean(centred * centred, axis=0, keepdims=True)
        normed = (centred * lax.rsqrt(spread + EPS) * ogain_v + obias_v).astype(BF16)
        val = lax.dot_general(normed, oweight[...], TN, preferred_element_type=F32)
        for g in range(2):
            update[pl.ds(g * JD + m, rows, stride=2 * PAD), :] = val[g * rows : (g + 1) * rows]

    for m in range(JD):
        finish(m)

    def write(g, carry):
        at = pl.ds(pl.multiple_of(g * wide, wide), wide)
        val = (update[at, :] * gate_val[at, :]).reshape(8, 2 * PAD, ch)
        out[pl.ds(pl.multiple_of(8 * g, 8), 8)] = val[:, : 2 * JD].astype(BF16)
        return carry

    lax.fori_loop(0, rows // 8, write, 0)

    forward_copy(0).wait_send()
    for d in range(1, n_pos):
        right_copy(d).wait_send()
        forward_copy(d).wait_send()
        target = xor(z, d, n_pos)

        @pl.when(relayed(z, target))
        def _():
            relay_copy(target).wait_send()

        @pl.when(jnp.logical_not(relayed(z, target)))
        def _():
            partial_copy(target).wait_send()


def on_device(pair, lengths, gain, bias, lg, lv, rg, rv, ogain, obias, ow, gw):
    rows, cols, ch = pair.shape
    hid = lg.shape[1]
    n_blk = lax.axis_size("blk")
    n_pos = lax.axis_size("chan")
    assert n_blk == 2 * n_pos and cols == 2 * rows and n_pos >= 4 and n_pos & (n_pos - 1) == 0
    slot_size = rows * n_blk // lengths.shape[0]
    vmem = pl.BlockSpec(memory_space=pltpu.VMEM)
    dma = pltpu.SemaphoreType.DMA((n_pos,))
    block = (JD * hid, cols)
    return pl.pallas_call(
        functools.partial(kernel, n_pos, slot_size),
        out_shape=jax.ShapeDtypeStruct((rows, 2 * JD, ch), BF16),
        in_specs=[pl.BlockSpec(memory_space=pltpu.SMEM), pl.BlockSpec(memory_space=pl.ANY)]
        + [vmem] * 10,
        out_specs=vmem,
        scratch_shapes=[
            pltpu.VMEM((rows, cols, ch), BF16),
            pltpu.VMEM((4 * hid, ch), BF16),
            pltpu.VMEM((n_blk,) + block, BF16),
            pltpu.VMEM((hid * (rows + 8), cols), F32),
            pltpu.VMEM((hid * (PAD + 8), cols), F32),
            pltpu.VMEM((hid * (PAD + 8), cols), F32),
            pltpu.VMEM((PAD * (hid + 8), 2 * rows), F32),
            pltpu.VMEM((n_pos,) + block, BF16),
            pltpu.VMEM(block, F32),
            pltpu.VMEM((n_pos,) + block, BF16),
            pltpu.VMEM((2 * rows * PAD, ch), F32),
            pltpu.VMEM((2 * rows * PAD, ch), F32),
            pltpu.VMEM((2 * rows * PAD, ch), F32),
            pltpu.SemaphoreType.DMA((2,)),
            dma,
            dma,
            dma,
            dma,
            dma,
            dma,
            pltpu.VMEM((n_pos,) + block, BF16),
            dma,
            dma,
        ],
        compiler_params=pltpu.CompilerParams(
            collective_id=0, has_side_effects=True, vmem_limit_bytes=60 * 2**20
        ),
    )(
        lengths,
        pair,
        gain.reshape(1, ch),
        bias.reshape(1, ch),
        lg,
        lv,
        rg,
        rv,
        ogain.reshape(1, hid),
        obias.reshape(1, hid),
        ow,
        gw,
    )


def solution(mesh):
    in_specs = (P("blk", "chan", None),) + (P(),) * 11
    out_specs = P("blk", "chan", None)
    return jax.shard_map(
        on_device, mesh=mesh, in_specs=in_specs, out_specs=out_specs, check_vma=False
    )
```

profile of v0, /device:TPU:7, one launch (start us, length us, event | category | flops | bytes accessed | tf_op | source)
XLA Modules:
  0.0 54.6 jit_solution(18087132121671675591)
XLA Ops:
  0.0 52.6 %shard_map.118 = bf16[64,26,128]{2,1,0:T(8,128)(2,1)} custom-call(s32[8]{0:T(128)} %lens.1, bf16[64,128,128]{2,1,0:T(8,128)(2,1)} %pair_hbm.1, f32[1,128]{1,0:T(1,128)} %bitcast.4, f32[1,128]{1,0:T(1,128)} %bitcast.5, bf16[128,128]{1,0:T(8,128)(2,1)} %lgate.1, bf16[128,128]{1,0:T(8,128)(2,1)} %lvalue.1, bf16[128,128]{1,0:T(8,128)(2,1)} %rgate.1, ...), custom_call_target="tpu_custom_call" | custom-call | tf_op jit(solution)/shard_map/pallas_call | solution.py:361
  52.6 2.0 %copy.13 = bf16[64,26,128]{2,0,1:T(8,128)(2,1)} copy(bf16[64,26,128]{2,1,0:T(8,128)(2,1)} %shard_map.118) | data formatting | bytes 851968 | tf_op jit(solution)/shard_map/pallas_call | solution.py:361
where the time goes:
time: 54.9 us; the launch traced here: 54.6 us
  Pallas kernels  52.6 us (96%)
  local copies, waits for them, and re-layouts  1.97 us (4%)
    pallas_call x1, Pallas kernels, on_device(): pl.pallas_call(functools.partial(kernel, n_pos, slot_size), out_shape=jax...  52.6 us
    pallas_call x1, local copies, waits for them, and re-layouts, on_device(): pl.pallas_call(functools.partial(kernel, n_pos, slot_size), out_shape=jax...  1.97 us

commit v1 on v0

v1 whole, which is shorter than its diff:
```python
import functools

import jax
import jax.numpy as jnp
from jax import lax
from jax.experimental import pallas as pl
from jax.experimental.pallas import tpu as pltpu
from jax.sharding import PartitionSpec as P

JD = 13
PAD = 16
CHUNKS = 4
LAG = 2
EPS = 1e-05
F32 = jnp.float32
BF16 = jnp.bfloat16
NT = (((1,), (1,)), ((), ()))
TN = (((0,), (0,)), ((), ()))
NN = (((1,), (0,)), ((), ()))


def xor(a, b, n):
    total, bit = 0, 1
    while bit < n:
        total = total + bit * ((a // bit + b // bit) % 2)
        bit *= 2
    return total


def reverse_bits(t, n):
    total, bit = 0, 1
    while bit < n:
        total = total + (n // 2 // bit) * ((t // bit) % 2)
        bit *= 2
    return total


def sigmoid(x):
    return 0.5 * jnp.tanh(0.5 * x) + 0.5


def layer_norm(x, gain, bias):
    centre = jnp.mean(x, axis=-1, keepdims=True)
    centred = x - centre
    spread = jnp.mean(centred * centred, axis=-1, keepdims=True)
    return centred * lax.rsqrt(spread + EPS) * gain + bias


def gray(t, n):
    return xor(t, t // 2, n)


def groups():
    ends = [-(-JD * i // CHUNKS) for i in range(CHUNKS + 1)]
    return [(a, b - a) for a, b in zip(ends[:-1], ends[1:])]


def kernel(
    n_pos,
    slot_size,
    lens_hbm,
    pair_hbm,
    gain_hbm,
    bias_hbm,
    lgate_hbm,
    lvalue_hbm,
    rgate_hbm,
    rvalue_hbm,
    ogain_hbm,
    obias_hbm,
    oweight_hbm,
    gweight_hbm,
    out_hbm,
    lens,
    vectors,
    raw,
    pair,
    weights,
    right_all,
    left,
    r0,
    r1,
    work,
    send,
    own,
    recv,
    relay,
    gate_in,
    gate_val,
    out,
    load_sem,
    out_sem,
    rs_send,
    rs_recv,
    fw_send,
    fw_recv,
    ps_send,
    ps_recv,
    rl_send,
    rl_recv,
):
    rows, cols, ch = pair.shape
    hid = raw.shape[2]
    part = hid // CHUNKS
    pitch = 2 * rows + 8
    total = n_pos * CHUNKS
    last = n_pos - 1
    half = n_pos // 2
    blk = lax.axis_index("blk")
    z = lax.axis_index("chan")
    q = blk // 2
    h = blk % 2
    partner = 2 * q + 1 - h

    def load(n, src, dst):
        copy = pltpu.make_async_copy(src, dst, load_sem.at[n])
        copy.start()
        return copy

    first = [
        load(0, pair_hbm.at[pl.ds(0, JD)], pair.at[pl.ds(0, JD)]),
        load(1, rgate_hbm, raw.at[0]),
        load(2, rvalue_hbm, raw.at[1]),
        load(3, gain_hbm, vectors.at[pl.ds(0, 1)]),
        load(4, bias_hbm, vectors.at[pl.ds(8, 1)]),
        load(5, lens_hbm, lens),
    ]
    second = [
        load(6, pair_hbm.at[pl.ds(JD, rows - JD)], pair.at[pl.ds(JD, rows - JD)]),
        load(7, lgate_hbm, raw.at[2]),
        load(8, lvalue_hbm, raw.at[3]),
    ]
    third = [
        load(9, gweight_hbm, raw.at[4]),
        load(10, oweight_hbm, raw.at[5]),
        load(11, ogain_hbm, vectors.at[pl.ds(16, 1)]),
        load(12, obias_hbm, vectors.at[pl.ds(24, 1)]),
    ]

    barrier = pltpu.get_barrier_semaphore()
    for d in range(1, n_pos):
        pl.semaphore_signal(barrier, inc=1, device_id={"blk": 2 * xor(q, d, n_pos) + h})
        pl.semaphore_signal(barrier, inc=1, device_id={"chan": xor(z, d, n_pos)})
    pl.semaphore_signal(barrier, inc=1, device_id={"blk": partner})

    def turn(n):
        weights[n * hid : (n + 1) * hid, :] = raw[n].astype(F32).T.astype(BF16)

    for copy in first:
        copy.wait()
    turn(0)
    turn(1)

    col = z * cols + lax.broadcasted_iota(jnp.int32, (1, cols), 1)
    chain = col // slot_size
    chain_len = jnp.zeros_like(col)
    for s in range(lens.shape[0]):
        chain_len = jnp.where(chain == s, lens[s], chain_len)
    col_real = (col % slot_size < chain_len).astype(F32)

    def row_real(i):
        pos = blk * rows + i
        return jnp.where(pos % slot_size < lens[pos // slot_size], 1.0, 0.0).astype(F32)

    gain_v, bias_v = vectors[0:1, :], vectors[8:9, :]

    def norm_rows(i, count):
        x = pair[pl.ds(i, count)].astype(F32).reshape(count * cols, ch)
        return layer_norm(x, gain_v, bias_v).astype(BF16)

    for m in range(JD):
        normed = norm_rows(m, 1)
        mix = lax.dot_general(weights[: 2 * hid, :], normed, NT, preferred_element_type=F32)
        val = sigmoid(mix[:hid]) * mix[hid:] * (col_real * row_real(m))
        for k in range(CHUNKS):
            right_all[blk, k, m * part : (m + 1) * part, :] = val[
                k * part : (k + 1) * part
            ].astype(BF16)

    pl.semaphore_wait(barrier, 2 * (n_pos - 1) + 1)

    def right_copy(d, k):
        return pltpu.make_async_remote_copy(
            src_ref=right_all.at[blk, k],
            dst_ref=right_all.at[blk, k],
            send_sem=rs_send.at[d, k],
            recv_sem=rs_recv.at[d, k],
            device_id={"blk": 2 * xor(q, d, n_pos) + h},
        )

    def forward_copy(d, k):
        mine = 2 * xor(q, d, n_pos) + h
        return pltpu.make_async_remote_copy(
            src_ref=right_all.at[mine, k],
            dst_ref=right_all.at[mine, k],
            send_sem=fw_send.at[d, k],
            recv_sem=fw_recv.at[d, k],
            device_id={"blk": partner},
        )

    for hops in range(1, n_pos.bit_length()):
        for k in range(CHUNKS):
            for d in range(1, n_pos):
                if bin(d).count("1") == hops:
                    right_copy(d, k).start()
            if hops == 1:
                forward_copy(0, k).start()

    for copy in second:
        copy.wait()
    turn(2)
    turn(3)

    def left_rows(t, carry):
        i = 8 * t
        normed = norm_rows(i, 8)
        for u in range(8):
            for g in range(2):
                gate_in[pl.ds(g * rows + i + u, JD, stride=pitch), :] = normed[
                    u * cols + g * rows : u * cols + g * rows + JD
                ].astype(F32)
        mix = lax.dot_general(weights[2 * hid :, :], normed, NT, preferred_element_type=F32)
        val = sigmoid(mix[:hid]) * mix[hid:]
        for u in range(8):
            left[pl.ds(i + u, hid, stride=rows + 8), :] = val[:, u * cols : (u + 1) * cols] * (
                col_real * row_real(i + u)
            )
        return carry

    lax.fori_loop(0, rows // 8, left_rows, 0)

    def partial_copy(p, k):
        e = xor(z, p, n_pos)
        return pltpu.make_async_remote_copy(
            src_ref=send.at[p, k],
            dst_ref=recv.at[e, k],
            send_sem=ps_send.at[e, k],
            recv_sem=ps_recv.at[e, k],
            device_id={"chan": p},
        )

    def group_copy(p, n):
        start, count = groups()[n]
        here = pl.ds(start * part, count * part)
        return pltpu.make_async_remote_copy(
            src_ref=send.at[p, :, here],
            dst_ref=recv.at[1, :, here],
            send_sem=ps_send.at[1, n],
            recv_sem=ps_recv.at[1, n],
            device_id={"chan": p},
        )

    def relayed(source, p):
        return ((source == 0) & (p >= half)) | ((source == last) & (p < half))

    next_in = jnp.where(z == 0, 1, jnp.where(z == last, last - 1, -1))
    behind = jnp.where(z == 1, 0, jnp.where(z == last - 1, last, -1))

    def relay_copy(p, k):
        return pltpu.make_async_remote_copy(
            src_ref=send.at[p, k],
            dst_ref=relay.at[p, k],
            send_sem=rl_send.at[p, k],
            recv_sem=rl_recv.at[p, k],
            device_id={"chan": jnp.where(z < half, 1, last - 1)},
        )

    same_side = q // half == z // half

    def distance(t):
        d = gray(t, n_pos)
        return jnp.where(same_side, reverse_bits(d, n_pos), d)

    lag = jnp.where(same_side, LAG, CHUNKS + LAG)

    def pass_on(s, on):
        k = s % CHUNKS
        p = xor(q, distance(s // CHUNKS), n_pos)

        @pl.when(on & relayed(behind, p))
        def _():
            relay_copy(p, k).wait_recv()
            send[p, k] = (send[p, k].astype(F32) + relay[p, k].astype(F32)).astype(BF16)
            partial_copy(p, k).start()

    far = distance(last)

    def step(s, carry):
        t = s // CHUNKS
        k = s % CHUNKS
        d = distance(t)
        p = xor(q, d, n_pos)

        @pl.when((t > 0) & (t < last))
        def _():
            right_copy(d, k).wait_recv()
            forward_copy(d, k).start()

        forward_copy(d, k).wait_recv()
        for g, dst in enumerate((r0, r1)):
            for m in range(JD):
                dst[pl.ds(m, part, stride=PAD + 8), :] = right_all[
                    2 * p + g, k, m * part : (m + 1) * part, :
                ].astype(F32)

        base = pl.multiple_of(k * part * (rows + 8), 8)
        for c in range(part):
            rr = slice(c * (PAD + 8), c * (PAD + 8) + PAD)
            lhs = jnp.concatenate([r0[rr, :], r1[rr, :]], axis=0).astype(BF16)
            lc = left[pl.ds(base + c * (rows + 8), rows), :].astype(BF16)
            o = lax.dot_general(lhs, lc, NT, preferred_element_type=F32)
            work[pl.ds(c, PAD, stride=part + 8), :] = jnp.concatenate([o[:PAD], o[PAD:]], axis=1)

        @pl.when(p == z)
        def _():
            for m in range(JD):
                own[k, m * part : (m + 1) * part, :] = work[
                    m * (part + 8) : m * (part + 8) + part, :
                ]

        @pl.when(p != z)
        def _():
            for m in range(JD):
                send[p, k, m * part : (m + 1) * part, :] = work[
                    m * (part + 8) : m * (part + 8) + part, :
                ].astype(BF16)

            @pl.when(relayed(z, p))
            def _():
                relay_copy(p, k).start()

            later = (p == next_in) | relayed(behind, p)

            @pl.when(jnp.logical_not(relayed(z, p) | later))
            def _():
                partial_copy(p, k).start()

        @pl.when(t == 1)
        def _():
            right_copy(far, k).wait_recv()
            forward_copy(far, k).start()

        before = jnp.maximum(s - lag, 0)
        pass_on(before, s >= lag)
        return carry

    lax.fori_loop(0, total, step, 0)

    @pl.when(next_in >= 0)
    def _():
        for n in range(CHUNKS):
            group_copy(next_in, n).start()

    def rest(j, carry):
        pass_on(total - CHUNKS - LAG + j, CHUNKS + LAG - j <= lag)
        return carry

    lax.fori_loop(0, CHUNKS + LAG, rest, 0)

    for copy in third:
        copy.wait()

    def gates(m, carry):
        mix = lax.dot_general(
            gate_in[pl.ds(pl.multiple_of(m * pitch, 8), 2 * rows), :].astype(BF16),
            raw[4],
            NN,
            preferred_element_type=F32,
        )
        gate_val[m] = sigmoid(mix)
        return carry

    lax.fori_loop(0, JD, gates, 0)

    ogain_v = jnp.broadcast_to(vectors[16:17, :], (2 * rows, hid)).T
    obias_v = jnp.broadcast_to(vectors[24:25, :], (2 * rows, hid)).T
    for e in range(2, n_pos):
        source = xor(z, e, n_pos)

        @pl.when(jnp.logical_not(relayed(source, z)))
        def _():
            def gather(k, carry):
                partial_copy(source, k).wait_recv()
                own[k] = own[k] + recv[e, k].astype(F32)
                return carry

            lax.fori_loop(0, CHUNKS, gather, 0)

    inner = behind >= 0

    @pl.when(jnp.logical_not(inner))
    def _():
        for k in range(CHUNKS):
            partial_copy(xor(z, 1, n_pos), k).wait_recv()

    def finish(m):
        here = slice(m * part, (m + 1) * part)
        total = jnp.concatenate(
            [own[k, here, :] + recv[1, k, here, :].astype(F32) for k in range(CHUNKS)], axis=0
        )
        total = total.astype(BF16).astype(F32)
        centred = total - jnp.mean(total, axis=0, keepdims=True)
        spread = jnp.mean(centred * centred, axis=0, keepdims=True)
        normed = (centred * lax.rsqrt(spread + EPS) * ogain_v + obias_v).astype(BF16)
        val = lax.dot_general(normed, raw[5], TN, preferred_element_type=F32)
        val = (val * gate_val[m]).astype(BF16)
        for g in range(2):
            out[g * JD + m] = val[g * rows : (g + 1) * rows]

    def out_copy(n, g):
        start, count = groups()[n]
        here = pl.ds(g * JD + start, count)
        return pltpu.make_async_copy(out.at[here], out_hbm.at[here], out_sem.at[g, n])

    for n, (start, count) in enumerate(groups()):

        @pl.when(inner)
        def _():
            group_copy(behind, n).wait_recv()

        for m in range(start, start + count):
            finish(m)
        for g in range(2):
            out_copy(n, g).start()

    for n in range(CHUNKS):
        for g in range(2):
            out_copy(n, g).wait()

    def drain(s, carry):
        d = s // CHUNKS
        k = s % CHUNKS
        forward_copy(d, k).wait_send()

        @pl.when(d > 0)
        def _():
            target = xor(z, d, n_pos)
            right_copy(d, k).wait_send()

            @pl.when(relayed(z, target))
            def _():
                relay_copy(target, k).wait_send()

            @pl.when(jnp.logical_not(relayed(z, target) | (target == next_in)))
            def _():
                partial_copy(target, k).wait_send()

        return carry

    lax.fori_loop(0, total, drain, 0)

    @pl.when(next_in >= 0)
    def _():
        for n in range(CHUNKS):
            group_copy(next_in, n).wait_send()


def on_device(pair, lengths, gain, bias, lg, lv, rg, rv, ogain, obias, ow, gw):
    rows, cols, ch = pair.shape
    hid = lg.shape[1]
    n_blk = lax.axis_size("blk")
    n_pos = lax.axis_size("chan")
    assert n_blk == 2 * n_pos and cols == 2 * rows and n_pos >= 4 and n_pos & (n_pos - 1) == 0
    slot_size = rows * n_blk // lengths.shape[0]
    part = hid // CHUNKS
    sems = pltpu.SemaphoreType.DMA((n_pos, CHUNKS))
    block = (CHUNKS, JD * part, cols)
    result = pl.pallas_call(
        functools.partial(kernel, n_pos, slot_size),
        out_shape=jax.ShapeDtypeStruct((2 * JD, rows, ch), BF16),
        in_specs=[pl.BlockSpec(memory_space=pl.ANY)] * 12,
        out_specs=pl.BlockSpec(memory_space=pl.ANY),
        scratch_shapes=[
            pltpu.SMEM(lengths.shape, jnp.int32),
            pltpu.VMEM((32, ch), F32),
            pltpu.VMEM((6, ch, hid), BF16),
            pltpu.VMEM((rows, cols, ch), BF16),
            pltpu.VMEM((4 * hid, ch), BF16),
            pltpu.VMEM((n_blk,) + block, BF16),
            pltpu.VMEM((hid * (rows + 8), cols), F32),
            pltpu.VMEM((part * (PAD + 8), cols), F32),
            pltpu.VMEM((part * (PAD + 8), cols), F32),
            pltpu.VMEM((PAD * (part + 8), 2 * rows), F32),
            pltpu.VMEM((n_pos,) + block, BF16),
            pltpu.VMEM(block, F32),
            pltpu.VMEM((n_pos,) + block, BF16),
            pltpu.VMEM((n_pos,) + block, BF16),
            pltpu.VMEM((PAD * (2 * rows + 8), ch), F32),
            pltpu.VMEM((JD, 2 * rows, ch), F32),
            pltpu.VMEM((2 * JD, rows, ch), BF16),
            pltpu.SemaphoreType.DMA((13,)),
            pltpu.SemaphoreType.DMA((2, CHUNKS)),
        ]
        + [sems] * 8,
        compiler_params=pltpu.CompilerParams(
            collective_id=0, has_side_effects=True, vmem_limit_bytes=60 * 2**20
        ),
    )(
        lengths,
        pair,
        gain.reshape(1, ch),
        bias.reshape(1, ch),
        lg,
        lv,
        rg,
        rv,
        ogain.reshape(1, hid),
        obias.reshape(1, hid),
        ow,
        gw,
    )
    return jnp.transpose(result, (1, 0, 2))


def solution(mesh):
    in_specs = (P("blk", "chan", None),) + (P(),) * 11
    out_specs = P("blk", "chan", None)
    return jax.shard_map(
        on_device, mesh=mesh, in_specs=in_specs, out_specs=out_specs, check_vma=False
    )
```

time: 54.9 us -> 51.9 us (0.945)
  the two profiles are of different devices: /device:TPU:7 before, /device:TPU:3 now
where the time goes in v1:
time: 51.9 us; the launch traced here: 51.7 us
  Pallas kernels  49.9 us (96%)
  local copies, waits for them, and re-layouts  1.79 us (3%)
    pallas_call x1, Pallas kernels, on_device(): pl.pallas_call(functools.partial(kernel, n_pos, slot_size), out_shape=jax...  49.9 us
    unnamed x1, local copies, waits for them, and re-layouts  1.79 us

profile of v1, /device:TPU:3, one launch (start us, length us, event | category | flops | bytes accessed | tf_op | source)
XLA Modules:
  0.0 51.7 jit_solution(17008298146841036571)
XLA Ops:
  0.0 49.9 %shard_map.118 = bf16[26,64,128]{2,1,0:T(8,128)(2,1)} custom-call(s32[8]{0:T(128)} %lens_hbm.1, bf16[64,128,128]{2,1,0:T(8,128)(2,1)} %pair_hbm.1, f32[1,128]{1,0:T(1,128)} %bitcast.6, f32[1,128]{1,0:T(1,128)} %bitcast.7, bf16[128,128]{1,0:T(8,128)(2,1)} %lgate_hbm.1, bf16[128,128]{1,0:T(8,128)(2,1)} %lvalue_hbm.1, bf16[128,128]{1,0:T(8,128)(2,1)} %rgate_hbm.1, ...), custom_call_target="tpu_custom_call" | custom-call | tf_op jit(solution)/shard_map/pallas_call | solution.py:468
  49.9 1.8 %copy.14 = bf16[64,26,128]{2,0,1:T(8,128)(2,1)} copy(bf16[64,26,128]{2,0,1:T(8,128)(2,1)} %bitcast.5) | data formatting | bytes 851968

commit v2 on v1

--- a/solution.py
+++ b/solution.py
@@ -10,7 +10,6 @@
 JD = 13
 PAD = 16
 CHUNKS = 4
-LAG = 2
 EPS = 1e-05
 F32 = jnp.float32
 BF16 = jnp.bfloat16
@@ -198,13 +197,10 @@
             device_id={"blk": partner},
         )
 
-    for hops in range(1, n_pos.bit_length()):
-        for k in range(CHUNKS):
-            for d in range(1, n_pos):
-                if bin(d).count("1") == hops:
-                    right_copy(d, k).start()
-            if hops == 1:
-                forward_copy(0, k).start()
+    for k in range(CHUNKS):
+        for d in sorted(range(1, n_pos), key=int.bit_count):
+            right_copy(d, k).start()
+        forward_copy(0, k).start()
 
     for copy in second:
         copy.wait()
@@ -267,15 +263,19 @@
 
     same_side = q // half == z // half
 
-    def distance(t):
-        d = gray(t, n_pos)
+    def side(d):
         return jnp.where(same_side, reverse_bits(d, n_pos), d)
 
-    lag = jnp.where(same_side, LAG, CHUNKS + LAG)
+    near, far = side(gray(1, n_pos)), side(gray(last, n_pos))
+
+    def place(s):
+        j = s % n_pos
+        t = jnp.where(j < 2, j, jnp.where(j == 2, last, j - 1))
+        return side(gray(t, n_pos)), s // n_pos
 
     def pass_on(s, on):
-        k = s % CHUNKS
-        p = xor(q, distance(s // CHUNKS), n_pos)
+        d, k = place(s)
+        p = xor(q, d, n_pos)
 
         @pl.when(on & relayed(behind, p))
         def _():
@@ -283,18 +283,23 @@
             send[p, k] = (send[p, k].astype(F32) + relay[p, k].astype(F32)).astype(BF16)
             partial_copy(p, k).start()
 
-    far = distance(last)
+    def share(d, k):
+        right_copy(d, k).wait_recv()
+        forward_copy(d, k).start()
 
     def step(s, carry):
-        t = s // CHUNKS
-        k = s % CHUNKS
-        d = distance(t)
+        d, k = place(s)
         p = xor(q, d, n_pos)
-
-        @pl.when((t > 0) & (t < last))
-        def _():
-            right_copy(d, k).wait_recv()
-            forward_copy(d, k).start()
+        opens = s % n_pos == 0
+
+        @pl.when(opens & same_side)
+        def _():
+            share(near, k)
+            share(far, k)
+
+        @pl.when(s % n_pos > 2)
+        def _():
+            share(d, k)
 
         forward_copy(d, k).wait_recv()
         for g, dst in enumerate((r0, r1)):
@@ -335,13 +340,12 @@
             def _():
                 partial_copy(p, k).start()
 
-        @pl.when(t == 1)
-        def _():
-            right_copy(far, k).wait_recv()
-            forward_copy(far, k).start()
-
-        before = jnp.maximum(s - lag, 0)
-        pass_on(before, s >= lag)
+        @pl.when(opens & jnp.logical_not(same_side))
+        def _():
+            share(near, k)
+            share(far, k)
+
+        pass_on(jnp.maximum(s - n_pos, 0), s >= n_pos)
         return carry
 
     lax.fori_loop(0, total, step, 0)
@@ -352,10 +356,10 @@
             group_copy(next_in, n).start()
 
     def rest(j, carry):
-        pass_on(total - CHUNKS - LAG + j, CHUNKS + LAG - j <= lag)
+        pass_on(total - n_pos + j, True)
         return carry
 
-    lax.fori_loop(0, CHUNKS + LAG, rest, 0)
+    lax.fori_loop(0, n_pos, rest, 0)
 
     for copy in third:
         copy.wait()
@@ -386,9 +390,9 @@
 
             lax.fori_loop(0, CHUNKS, gather, 0)
 
-    inner = behind >= 0
-
-    @pl.when(jnp.logical_not(inner))
+    fed = behind >= 0
+
+    @pl.when(jnp.logical_not(fed))
     def _():
         for k in range(CHUNKS):
             partial_copy(xor(z, 1, n_pos), k).wait_recv()
@@ -414,7 +418,7 @@
 
     for n, (start, count) in enumerate(groups()):
 
-        @pl.when(inner)
+        @pl.when(fed)
         def _():
             group_copy(behind, n).wait_recv()
 

time: 51.9 us -> 46.6 us (0.90)
  the two profiles are of different devices: /device:TPU:3 before, /device:TPU:10 now
where the time goes in v2:
time: 46.6 us; the launch traced here: 46.4 us
  Pallas kernels  44.6 us (96%)
  local copies, waits for them, and re-layouts  1.79 us (4%)
    pallas_call x1, Pallas kernels, on_device(): pl.pallas_call(functools.partial(kernel, n_pos, slot_size), out_shape=jax...  44.6 us
    unnamed x1, local copies, waits for them, and re-layouts  1.79 us

profile of v2, /device:TPU:10, one launch (start us, length us, event | category | flops | bytes accessed | tf_op | source)
XLA Modules:
  0.0 46.4 jit_solution(12860909985812316145)
XLA Ops:
  0.0 44.6 %shard_map.118 = bf16[26,64,128]{2,1,0:T(8,128)(2,1)} custom-call(s32[8]{0:T(128)} %lens_hbm.1, bf16[64,128,128]{2,1,0:T(8,128)(2,1)} %pair_hbm.1, f32[1,128]{1,0:T(1,128)} %bitcast.6, f32[1,128]{1,0:T(1,128)} %bitcast.7, bf16[128,128]{1,0:T(8,128)(2,1)} %lgate_hbm.1, bf16[128,128]{1,0:T(8,128)(2,1)} %lvalue_hbm.1, bf16[128,128]{1,0:T(8,128)(2,1)} %rgate_hbm.1, ...), custom_call_target="tpu_custom_call" | custom-call | tf_op jit(solution)/shard_map/pallas_call | solution.py:472
  44.6 1.8 %copy.14 = bf16[64,26,128]{2,0,1:T(8,128)(2,1)} copy(bf16[64,26,128]{2,0,1:T(8,128)(2,1)} %bitcast.5) | data formatting | bytes 851968

commit v3 on v2

--- a/solution.py
+++ b/solution.py
@@ -10,6 +10,7 @@
 JD = 13
 PAD = 16
 CHUNKS = 4
+HOLD = 1
 EPS = 1e-05
 F32 = jnp.float32
 BF16 = jnp.bfloat16
@@ -69,7 +70,7 @@
     obias_hbm,
     oweight_hbm,
     gweight_hbm,
-    out_hbm,
+    out,
     lens,
     vectors,
     raw,
@@ -86,16 +87,11 @@
     relay,
     gate_in,
     gate_val,
-    out,
     load_sem,
-    out_sem,
-    rs_send,
+    sent,
     rs_recv,
-    fw_send,
     fw_recv,
-    ps_send,
     ps_recv,
-    rl_send,
     rl_recv,
 ):
     rows, cols, ch = pair.shape
@@ -143,7 +139,7 @@
     pl.semaphore_signal(barrier, inc=1, device_id={"blk": partner})
 
     def turn(n):
-        weights[n * hid : (n + 1) * hid, :] = raw[n].astype(F32).T.astype(BF16)
+        weights[n * hid : (n + 1) * hid, :] = (0.5 * raw[n].astype(F32)).T.astype(BF16)
 
     for copy in first:
         copy.wait()
@@ -161,20 +157,26 @@
         pos = blk * rows + i
         return jnp.where(pos % slot_size < lens[pos // slot_size], 1.0, 0.0).astype(F32)
 
-    gain_v, bias_v = vectors[0:1, :], vectors[8:9, :]
-
-    def norm_rows(i, count):
-        x = pair[pl.ds(i, count)].astype(F32).reshape(count * cols, ch)
-        return layer_norm(x, gain_v, bias_v).astype(BF16)
-
+    gain_v, bias_v = vectors[0:1, :] * ch**0.5, vectors[8:9, :]
+    average = jnp.full((ch, ch), 1.0 / ch, BF16)
+
+    def norm_rows(i, count, by_matmul):
+        x = pair[pl.ds(i, count)].reshape(count * cols, ch)
+        if by_matmul:
+            centre = lax.dot_general(x, average, NN, preferred_element_type=F32)
+        else:
+            centre = jnp.mean(x.astype(F32), axis=-1, keepdims=True)
+        centred = x.astype(F32) - centre
+        spread = jnp.sum(centred * centred, axis=-1, keepdims=True)
+        return (centred * lax.rsqrt(spread + ch * EPS) * gain_v + bias_v).astype(BF16)
+
+    normed = norm_rows(0, JD, True)
+    mix = lax.dot_general(weights[: 2 * hid, :], normed, NT, preferred_element_type=F32)
+    val = (jnp.tanh(mix[:hid]) + 1.0) * mix[hid:]
     for m in range(JD):
-        normed = norm_rows(m, 1)
-        mix = lax.dot_general(weights[: 2 * hid, :], normed, NT, preferred_element_type=F32)
-        val = sigmoid(mix[:hid]) * mix[hid:] * (col_real * row_real(m))
+        row = (val[:, m * cols : (m + 1) * cols] * (col_real * row_real(m))).astype(BF16)
         for k in range(CHUNKS):
-            right_all[blk, k, m * part : (m + 1) * part, :] = val[
-                k * part : (k + 1) * part
-            ].astype(BF16)
+            right_all[blk, k, m * part : (m + 1) * part, :] = row[k * part : (k + 1) * part]
 
     pl.semaphore_wait(barrier, 2 * (n_pos - 1) + 1)
 
@@ -182,7 +184,7 @@
         return pltpu.make_async_remote_copy(
             src_ref=right_all.at[blk, k],
             dst_ref=right_all.at[blk, k],
-            send_sem=rs_send.at[d, k],
+            send_sem=sent.at[0],
             recv_sem=rs_recv.at[d, k],
             device_id={"blk": 2 * xor(q, d, n_pos) + h},
         )
@@ -192,15 +194,23 @@
         return pltpu.make_async_remote_copy(
             src_ref=right_all.at[mine, k],
             dst_ref=right_all.at[mine, k],
-            send_sem=fw_send.at[d, k],
+            send_sem=sent.at[1],
             recv_sem=fw_recv.at[d, k],
             device_id={"blk": partner},
         )
 
-    for k in range(CHUNKS):
-        for d in sorted(range(1, n_pos), key=int.bit_count):
-            right_copy(d, k).start()
-        forward_copy(0, k).start()
+    hops = sorted(range(1, n_pos), key=int.bit_count)
+    close = n_pos.bit_length() - 1
+    for d in hops[:close]:
+        right_copy(d, 0).start()
+    forward_copy(0, 0).start()
+
+    def send_rest():
+        for k in range(CHUNKS):
+            for d in hops[close if k == 0 else 0 :]:
+                right_copy(d, k).start()
+            if k > 0:
+                forward_copy(0, k).start()
 
     for copy in second:
         copy.wait()
@@ -208,30 +218,35 @@
     turn(3)
 
     def left_rows(t, carry):
-        i = 8 * t
-        normed = norm_rows(i, 8)
-        for u in range(8):
+        i = 16 * t
+        normed = norm_rows(i, 16, True)
+        for u in range(16):
             for g in range(2):
                 gate_in[pl.ds(g * rows + i + u, JD, stride=pitch), :] = normed[
                     u * cols + g * rows : u * cols + g * rows + JD
                 ].astype(F32)
         mix = lax.dot_general(weights[2 * hid :, :], normed, NT, preferred_element_type=F32)
-        val = sigmoid(mix[:hid]) * mix[hid:]
-        for u in range(8):
+        val = (jnp.tanh(mix[:hid]) + 1.0) * mix[hid:]
+        for u in range(16):
             left[pl.ds(i + u, hid, stride=rows + 8), :] = val[:, u * cols : (u + 1) * cols] * (
                 col_real * row_real(i + u)
             )
+
+        @pl.when(t == HOLD)
+        def _():
+            send_rest()
+
         return carry
 
-    lax.fori_loop(0, rows // 8, left_rows, 0)
+    lax.fori_loop(0, rows // 16, left_rows, 0)
 
     def partial_copy(p, k):
         e = xor(z, p, n_pos)
         return pltpu.make_async_remote_copy(
             src_ref=send.at[p, k],
             dst_ref=recv.at[e, k],
-            send_sem=ps_send.at[e, k],
-            recv_sem=ps_recv.at[e, k],
+            send_sem=sent.at[2],
+            recv_sem=ps_recv.at[jnp.where(e == 1, n_pos + k, e)],
             device_id={"chan": p},
         )
 
@@ -241,8 +256,8 @@
         return pltpu.make_async_remote_copy(
             src_ref=send.at[p, :, here],
             dst_ref=recv.at[1, :, here],
-            send_sem=ps_send.at[1, n],
-            recv_sem=ps_recv.at[1, n],
+            send_sem=sent.at[2],
+            recv_sem=ps_recv.at[n_pos + n],
             device_id={"chan": p},
         )
 
@@ -256,8 +271,8 @@
         return pltpu.make_async_remote_copy(
             src_ref=send.at[p, k],
             dst_ref=relay.at[p, k],
-            send_sem=rl_send.at[p, k],
-            recv_sem=rl_recv.at[p, k],
+            send_sem=sent.at[2],
+            recv_sem=rl_recv.at[p % half, k],
             device_id={"chan": jnp.where(z < half, 1, last - 1)},
         )
 
@@ -383,8 +398,15 @@
 
         @pl.when(jnp.logical_not(relayed(source, z)))
         def _():
+            pltpu.make_async_remote_copy(
+                src_ref=send.at[source],
+                dst_ref=recv.at[e],
+                send_sem=sent.at[2],
+                recv_sem=ps_recv.at[e],
+                device_id={"chan": source},
+            ).wait_recv()
+
             def gather(k, carry):
-                partial_copy(source, k).wait_recv()
                 own[k] = own[k] + recv[e, k].astype(F32)
                 return carry
 
@@ -411,11 +433,6 @@
         for g in range(2):
             out[g * JD + m] = val[g * rows : (g + 1) * rows]
 
-    def out_copy(n, g):
-        start, count = groups()[n]
-        here = pl.ds(g * JD + start, count)
-        return pltpu.make_async_copy(out.at[here], out_hbm.at[here], out_sem.at[g, n])
-
     for n, (start, count) in enumerate(groups()):
 
         @pl.when(fed)
@@ -424,39 +441,19 @@
 
         for m in range(start, start + count):
             finish(m)
-        for g in range(2):
-            out_copy(n, g).start()
-
-    for n in range(CHUNKS):
-        for g in range(2):
-            out_copy(n, g).wait()
-
-    def drain(s, carry):
-        d = s // CHUNKS
-        k = s % CHUNKS
-        forward_copy(d, k).wait_send()
-
-        @pl.when(d > 0)
-        def _():
-            target = xor(z, d, n_pos)
-            right_copy(d, k).wait_send()
-
-            @pl.when(relayed(z, target))
-            def _():
-                relay_copy(target, k).wait_send()
-
-            @pl.when(jnp.logical_not(relayed(z, target) | (target == next_in)))
-            def _():
-                partial_copy(target, k).wait_send()
-
-        return carry
-
-    lax.fori_loop(0, total, drain, 0)
-
-    @pl.when(next_in >= 0)
-    def _():
-        for n in range(CHUNKS):
-            group_copy(next_in, n).wait_send()
+    def drain(n, blocks, buffer):
+        here = buffer.at[pl.ds(0, blocks)]
+        pltpu.make_async_remote_copy(
+            src_ref=here,
+            dst_ref=here,
+            send_sem=sent.at[n],
+            recv_sem=ps_recv.at[0],
+            device_id={"blk": partner},
+        ).wait_send()
+
+    drain(0, n_pos - 1, right_all)
+    drain(1, n_pos, right_all)
+    drain(2, n_pos - 1, send)
 
 
 def on_device(pair, lengths, gain, bias, lg, lv, rg, rv, ogain, obias, ow, gw):
@@ -467,13 +464,26 @@
     assert n_blk == 2 * n_pos and cols == 2 * rows and n_pos >= 4 and n_pos & (n_pos - 1) == 0
     slot_size = rows * n_blk // lengths.shape[0]
     part = hid // CHUNKS
-    sems = pltpu.SemaphoreType.DMA((n_pos, CHUNKS))
     block = (CHUNKS, JD * part, cols)
+    operands = (
+        lengths,
+        pair,
+        gain.reshape(1, ch),
+        bias.reshape(1, ch),
+        lg,
+        lv,
+        rg,
+        rv,
+        ogain.reshape(1, hid),
+        obias.reshape(1, hid),
+        ow,
+        gw,
+    )
     result = pl.pallas_call(
         functools.partial(kernel, n_pos, slot_size),
         out_shape=jax.ShapeDtypeStruct((2 * JD, rows, ch), BF16),
         in_specs=[pl.BlockSpec(memory_space=pl.ANY)] * 12,
-        out_specs=pl.BlockSpec(memory_space=pl.ANY),
+        out_specs=pl.BlockSpec(memory_space=pltpu.VMEM),
         scratch_shapes=[
             pltpu.SMEM(lengths.shape, jnp.int32),
             pltpu.VMEM((32, ch), F32),
@@ -491,28 +501,19 @@
             pltpu.VMEM((n_pos,) + block, BF16),
             pltpu.VMEM((PAD * (2 * rows + 8), ch), F32),
             pltpu.VMEM((JD, 2 * rows, ch), F32),
-            pltpu.VMEM((2 * JD, rows, ch), BF16),
             pltpu.SemaphoreType.DMA((13,)),
-            pltpu.SemaphoreType.DMA((2, CHUNKS)),
-        ]
-        + [sems] * 8,
+            pltpu.SemaphoreType.DMA((3,)),
+            pltpu.SemaphoreType.DMA((n_pos, CHUNKS)),
+            pltpu.SemaphoreType.DMA((n_pos, CHUNKS)),
+            pltpu.SemaphoreType.DMA((n_pos + CHUNKS,)),
+            pltpu.SemaphoreType.DMA((n_pos // 2, CHUNKS)),
+        ],
         compiler_params=pltpu.CompilerParams(
-            collective_id=0, has_side_effects=True, vmem_limit_bytes=60 * 2**20
+            collective_id=0,
+            has_side_effects=True,
+            vmem_limit_bytes=(n_blk + 3 * n_pos) * 2 * JD * hid * cols + 16 * 2**20,
         ),
-    )(
-        lengths,
-        pair,
-        gain.reshape(1, ch),
-        bias.reshape(1, ch),
-        lg,
-        lv,
-        rg,
-        rv,
-        ogain.reshape(1, hid),
-        obias.reshape(1, hid),
-        ow,
-        gw,
-    )
+    )(*[pltpu.with_memory_space_constraint(x, pltpu.HBM) for x in operands])
     return jnp.transpose(result, (1, 0, 2))
 
 

time: 46.6 us -> 42.9 us (0.921)
  Pallas kernels: 44.6 us -> 42 us
  local copies, waits for them, and re-layouts: 1.79 us -> 0.76 us
    pallas_call x1, Pallas kernels: 44.6 us -> 42 us  [on_device(): pl.pallas_call(functools.partial(kernel, n_pos, slot_size), out_shape=jax...]
    unnamed x1, local copies, waits for them, and re-layouts: 1.79 us -> 0.76 us
where the time goes in v3:
time: 42.9 us; the launch traced here: 42.8 us
  Pallas kernels  42 us (98%)
  local copies, waits for them, and re-layouts  0.76 us (2%)
    pallas_call x1, Pallas kernels, on_device(): pl.pallas_call(functools.partial(kernel, n_pos, slot_size), out_shape=jax...  42 us

profile of v3, /device:TPU:10, one launch (start us, length us, event | category | flops | bytes accessed | tf_op | source)
XLA Modules:
  0.0 42.8 jit_solution(5217556121281714054)
XLA Ops:
  0.0 42.0 %shard_map.118 = bf16[26,64,128]{2,1,0:T(8,128)(2,1)S(1)} custom-call(s32[8]{0:T(128)} %lens_hbm.1, bf16[64,128,128]{2,1,0:T(8,128)(2,1)} %pair_hbm.1, f32[1,128]{1,0:T(1,128)} %bitcast.6, f32[1,128]{1,0:T(1,128)} %bitcast.7, bf16[128,128]{1,0:T(8,128)(2,1)} %lgate_hbm.1, bf16[128,128]{1,0:T(8,128)(2,1)} %lvalue_hbm.1, bf16[128,128]{1,0:T(8,128)(2,1)} %rgate_hbm.1, ...), custom_call_target="tpu_custom_call" | custom-call | tf_op jit(solution)/shard_map/pallas_call | solution.py:482
  42.0 0.8 %copy.14 = bf16[64,26,128]{2,0,1:T(8,128)(2,1)} copy(bf16[64,26,128]{2,0,1:T(8,128)(2,1)S(1)} %bitcast.5) | data formatting | bytes 851968

commit v4 on v3

--- a/solution.py
+++ b/solution.py
@@ -50,9 +50,7 @@
     return xor(t, t // 2, n)
 
 
-def groups():
-    ends = [-(-JD * i // CHUNKS) for i in range(CHUNKS + 1)]
-    return [(a, b - a) for a, b in zip(ends[:-1], ends[1:])]
+GROUPS = ((0, 5), (5, 5), (10, 3))
 
 
 def kernel(
@@ -251,13 +249,13 @@
         )
 
     def group_copy(p, n):
-        start, count = groups()[n]
+        start, count = GROUPS[n]
         here = pl.ds(start * part, count * part)
         return pltpu.make_async_remote_copy(
-            src_ref=send.at[p, :, here],
-            dst_ref=recv.at[1, :, here],
+            src_ref=send.at[p, pl.ds(1, CHUNKS - 1), here],
+            dst_ref=recv.at[1, pl.ds(1, CHUNKS - 1), here],
             send_sem=sent.at[2],
-            recv_sem=ps_recv.at[n_pos + n],
+            recv_sem=ps_recv.at[n_pos + 1 + n],
             device_id={"chan": p},
         )
 
@@ -285,6 +283,7 @@
 
     def place(s):
         j = s % n_pos
+        j = jnp.where((j < 3) & (q == z), (j + 1) % 3, j)
         t = jnp.where(j < 2, j, jnp.where(j == 2, last, j - 1))
         return side(gray(t, n_pos)), s // n_pos
 
@@ -307,7 +306,7 @@
         p = xor(q, d, n_pos)
         opens = s % n_pos == 0
 
-        @pl.when(opens & same_side)
+        @pl.when(opens & (q == z))
         def _():
             share(near, k)
             share(far, k)
@@ -349,13 +348,13 @@
             def _():
                 relay_copy(p, k).start()
 
-            later = (p == next_in) | relayed(behind, p)
+            later = ((p == next_in) & (k > 0)) | relayed(behind, p)
 
             @pl.when(jnp.logical_not(relayed(z, p) | later))
             def _():
                 partial_copy(p, k).start()
 
-        @pl.when(opens & jnp.logical_not(same_side))
+        @pl.when(opens & (q != z))
         def _():
             share(near, k)
             share(far, k)
@@ -367,7 +366,7 @@
 
     @pl.when(next_in >= 0)
     def _():
-        for n in range(CHUNKS):
+        for n in range(len(GROUPS)):
             group_copy(next_in, n).start()
 
     def rest(j, carry):
@@ -433,7 +432,11 @@
         for g in range(2):
             out[g * JD + m] = val[g * rows : (g + 1) * rows]
 
-    for n, (start, count) in enumerate(groups()):
+    @pl.when(fed)
+    def _():
+        partial_copy(behind, 0).wait_recv()
+
+    for n, (start, count) in enumerate(GROUPS):
 
         @pl.when(fed)
         def _():

time: 42.9 us -> 40.8 us (0.951)
  Pallas kernels: 42 us -> 39.8 us
    pallas_call x1, Pallas kernels: 42 us -> 39.8 us  [on_device(): pl.pallas_call(functools.partial(kernel, n_pos, slot_size), out_shape=jax...]
where the time goes in v4:
time: 40.8 us; the launch traced here: 40.5 us
  Pallas kernels  39.8 us (98%)
  local copies, waits for them, and re-layouts  0.76 us (2%)
    pallas_call x1, Pallas kernels, on_device(): pl.pallas_call(functools.partial(kernel, n_pos, slot_size), out_shape=jax...  39.8 us

profile of v4, /device:TPU:10, one launch (start us, length us, event | category | flops | bytes accessed | tf_op | source)
XLA Modules:
  0.0 40.5 jit_solution(7629037728407472166)
XLA Ops:
  0.0 39.8 %shard_map.118 = bf16[26,64,128]{2,1,0:T(8,128)(2,1)S(1)} custom-call(s32[8]{0:T(128)} %lens_hbm.1, bf16[64,128,128]{2,1,0:T(8,128)(2,1)} %pair_hbm.1, f32[1,128]{1,0:T(1,128)} %bitcast.6, f32[1,128]{1,0:T(1,128)} %bitcast.7, bf16[128,128]{1,0:T(8,128)(2,1)} %lgate_hbm.1, bf16[128,128]{1,0:T(8,128)(2,1)} %lvalue_hbm.1, bf16[128,128]{1,0:T(8,128)(2,1)} %rgate_hbm.1, ...), custom_call_target="tpu_custom_call" | custom-call | tf_op jit(solution)/shard_map/pallas_call | solution.py:485
  39.8 0.8 %copy.14 = bf16[64,26,128]{2,0,1:T(8,128)(2,1)} copy(bf16[64,26,128]{2,0,1:T(8,128)(2,1)S(1)} %bitcast.5) | data formatting | bytes 851968

commit v5 on v4

--- a/solution.py
+++ b/solution.py
@@ -91,6 +91,7 @@
     fw_recv,
     ps_recv,
     rl_recv,
+    ready,
 ):
     rows, cols, ch = pair.shape
     hid = raw.shape[2]
@@ -130,10 +131,25 @@
         load(12, obias_hbm, vectors.at[pl.ds(24, 1)]),
     ]
 
+    def relayed(source, p):
+        return ((source == 0) & (p >= half)) | ((source == last) & (p < half))
+
+    def across(source, p):
+        return ((source == 1) & (p == last)) | ((source == last - 1) & (p == 0))
+
+    next_in = jnp.where(z == 0, 1, jnp.where(z == last, last - 1, -1))
+    behind = jnp.where(z == 1, 0, jnp.where(z == last - 1, last, -1))
+
+    fed = behind >= 0
     barrier = pltpu.get_barrier_semaphore()
     for d in range(1, n_pos):
         pl.semaphore_signal(barrier, inc=1, device_id={"blk": 2 * xor(q, d, n_pos) + h})
-        pl.semaphore_signal(barrier, inc=1, device_id={"chan": xor(z, d, n_pos)})
+        source = xor(z, d, n_pos)
+
+        @pl.when(jnp.logical_not(relayed(source, z) | across(source, z)))
+        def _():
+            pl.semaphore_signal(barrier, inc=1, device_id={"chan": source})
+
     pl.semaphore_signal(barrier, inc=1, device_id={"blk": partner})
 
     def turn(n):
@@ -176,7 +192,13 @@
         for k in range(CHUNKS):
             right_all[blk, k, m * part : (m + 1) * part, :] = row[k * part : (k + 1) * part]
 
-    pl.semaphore_wait(barrier, 2 * (n_pos - 1) + 1)
+    direct = jnp.where(next_in >= 0, half - 1, jnp.where(fed, last - 1, last))
+    pl.semaphore_wait(barrier, direct + n_pos)
+
+    @pl.when(fed)
+    def _():
+        pl.semaphore_signal(ready, inc=1, device_id={"chan": last - z})
+
 
     def right_copy(d, k):
         return pltpu.make_async_remote_copy(
@@ -238,6 +260,10 @@
 
     lax.fori_loop(0, rows // 16, left_rows, 0)
 
+    @pl.when(fed)
+    def _():
+        pl.semaphore_wait(ready, 1)
+
     def partial_copy(p, k):
         e = xor(z, p, n_pos)
         return pltpu.make_async_remote_copy(
@@ -259,12 +285,6 @@
             device_id={"chan": p},
         )
 
-    def relayed(source, p):
-        return ((source == 0) & (p >= half)) | ((source == last) & (p < half))
-
-    next_in = jnp.where(z == 0, 1, jnp.where(z == last, last - 1, -1))
-    behind = jnp.where(z == 1, 0, jnp.where(z == last - 1, last, -1))
-
     def relay_copy(p, k):
         return pltpu.make_async_remote_copy(
             src_ref=send.at[p, k],
@@ -348,7 +368,7 @@
             def _():
                 relay_copy(p, k).start()
 
-            later = ((p == next_in) & (k > 0)) | relayed(behind, p)
+            later = ((p == next_in) & ((k > 0) | jnp.logical_not(same_side))) | relayed(behind, p)
 
             @pl.when(jnp.logical_not(relayed(z, p) | later))
             def _():
@@ -357,12 +377,23 @@
         @pl.when(opens & (q != z))
         def _():
             share(near, k)
-            share(far, k)
+
+            @pl.when(k > 0)
+            def _():
+                share(far, k)
+
+        @pl.when((s == 1) & (q != z))
+        def _():
+            share(far, 0)
 
         pass_on(jnp.maximum(s - n_pos, 0), s >= n_pos)
         return carry
 
     lax.fori_loop(0, total, step, 0)
+
+    @pl.when((next_in >= 0) & jnp.logical_not(same_side))
+    def _():
+        partial_copy(next_in, 0).start()
 
     @pl.when(next_in >= 0)
     def _():
@@ -410,8 +441,6 @@
                 return carry
 
             lax.fori_loop(0, CHUNKS, gather, 0)
-
-    fed = behind >= 0
 
     @pl.when(jnp.logical_not(fed))
     def _():
@@ -510,6 +539,7 @@
             pltpu.SemaphoreType.DMA((n_pos, CHUNKS)),
             pltpu.SemaphoreType.DMA((n_pos + CHUNKS,)),
             pltpu.SemaphoreType.DMA((n_pos // 2, CHUNKS)),
+            pltpu.SemaphoreType.REGULAR,
         ],
         compiler_params=pltpu.CompilerParams(
             collective_id=0,

time: 40.8 us -> 40.3 us (0.988); the launches traced: 40.5 us -> 39.6 us
  Pallas kernels: 39.8 us -> 38.8 us
    pallas_call x1, Pallas kernels: 39.8 us -> 38.8 us  [on_device(): pl.pallas_call(functools.partial(kernel, n_pos, slot_size), out_shape=jax...]
where the time goes in v5:
time: 40.3 us; the launch traced here: 39.6 us
  Pallas kernels  38.8 us (96%)
  local copies, waits for them, and re-layouts  0.76 us (2%)
    pallas_call x1, Pallas kernels, on_device(): pl.pallas_call(functools.partial(kernel, n_pos, slot_size), out_shape=jax...  38.8 us

profile of v5, /device:TPU:10, one launch (start us, length us, event | category | flops | bytes accessed | tf_op | source)
XLA Modules:
  0.0 39.6 jit_solution(3957125779989192529)
XLA Ops:
  0.0 38.8 %shard_map.118 = bf16[26,64,128]{2,1,0:T(8,128)(2,1)S(1)} custom-call(s32[8]{0:T(128)} %lens_hbm.1, bf16[64,128,128]{2,1,0:T(8,128)(2,1)} %pair_hbm.1, f32[1,128]{1,0:T(1,128)} %bitcast.6, f32[1,128]{1,0:T(1,128)} %bitcast.7, bf16[128,128]{1,0:T(8,128)(2,1)} %lgate_hbm.1, bf16[128,128]{1,0:T(8,128)(2,1)} %lvalue_hbm.1, bf16[128,128]{1,0:T(8,128)(2,1)} %rgate_hbm.1, ...), custom_call_target="tpu_custom_call" | custom-call | tf_op jit(solution)/shard_map/pallas_call | solution.py:514
  38.8 0.8 %copy.14 = bf16[64,26,128]{2,0,1:T(8,128)(2,1)} copy(bf16[64,26,128]{2,0,1:T(8,128)(2,1)S(1)} %bitcast.5) | data formatting | bytes 851968

commit v6 on v5

--- a/solution.py
+++ b/solution.py
@@ -119,6 +119,32 @@
         load(4, bias_hbm, vectors.at[pl.ds(8, 1)]),
         load(5, lens_hbm, lens),
     ]
+    def relayed(source, p):
+        return ((source == 0) & (p >= half)) | ((source == last) & (p < half))
+
+    def across(source, p):
+        return ((source == 1) & (p == last)) | ((source == last - 1) & (p == 0))
+
+    next_in = jnp.where(z == 0, 1, jnp.where(z == last, last - 1, -1))
+    behind = jnp.where(z == 1, 0, jnp.where(z == last - 1, last, -1))
+
+    fed = behind >= 0
+    barrier = pltpu.get_barrier_semaphore()
+    for d in range(1, n_pos):
+        pl.semaphore_signal(barrier, inc=1, device_id={"blk": 2 * xor(q, d, n_pos) + h})
+        source = xor(z, d, n_pos)
+
+        @pl.when(jnp.logical_not(relayed(source, z) | across(source, z)))
+        def _():
+            pl.semaphore_signal(barrier, inc=1, device_id={"chan": source})
+
+    pl.semaphore_signal(barrier, inc=1, device_id={"blk": partner})
+
+    def turn(n):
+        weights[n * hid : (n + 1) * hid, :] = (0.5 * raw[n].astype(F32)).T.astype(BF16)
+
+    for copy in first:
+        copy.wait()
     second = [
         load(6, pair_hbm.at[pl.ds(JD, rows - JD)], pair.at[pl.ds(JD, rows - JD)]),
         load(7, lgate_hbm, raw.at[2]),
@@ -130,33 +156,6 @@
         load(11, ogain_hbm, vectors.at[pl.ds(16, 1)]),
         load(12, obias_hbm, vectors.at[pl.ds(24, 1)]),
     ]
-
-    def relayed(source, p):
-        return ((source == 0) & (p >= half)) | ((source == last) & (p < half))
-
-    def across(source, p):
-        return ((source == 1) & (p == last)) | ((source == last - 1) & (p == 0))
-
-    next_in = jnp.where(z == 0, 1, jnp.where(z == last, last - 1, -1))
-    behind = jnp.where(z == 1, 0, jnp.where(z == last - 1, last, -1))
-
-    fed = behind >= 0
-    barrier = pltpu.get_barrier_semaphore()
-    for d in range(1, n_pos):
-        pl.semaphore_signal(barrier, inc=1, device_id={"blk": 2 * xor(q, d, n_pos) + h})
-        source = xor(z, d, n_pos)
-
-        @pl.when(jnp.logical_not(relayed(source, z) | across(source, z)))
-        def _():
-            pl.semaphore_signal(barrier, inc=1, device_id={"chan": source})
-
-    pl.semaphore_signal(barrier, inc=1, device_id={"blk": partner})
-
-    def turn(n):
-        weights[n * hid : (n + 1) * hid, :] = (0.5 * raw[n].astype(F32)).T.astype(BF16)
-
-    for copy in first:
-        copy.wait()
     turn(0)
     turn(1)
 

time: 40.3 us -> 40.2 us (level)
  the two profiles are of different devices: /device:TPU:10 before, /device:TPU:17 now
where the time goes in v6:
time: 40.2 us; the launch traced here: 40 us
  Pallas kernels  39.3 us (98%)
  local copies, waits for them, and re-layouts  0.76 us (2%)
    pallas_call x1, Pallas kernels, on_device(): pl.pallas_call(functools.partial(kernel, n_pos, slot_size), out_shape=jax...  39.3 us

profile of v6, /device:TPU:17, one launch (start us, length us, event | category | flops | bytes accessed | tf_op | source)
XLA Modules:
  0.0 40.0 jit_solution(11978116308706985025)
XLA Ops:
  0.0 39.3 %shard_map.118 = bf16[26,64,128]{2,1,0:T(8,128)(2,1)S(1)} custom-call(s32[8]{0:T(128)} %lens_hbm.1, bf16[64,128,128]{2,1,0:T(8,128)(2,1)} %pair_hbm.1, f32[1,128]{1,0:T(1,128)} %bitcast.6, f32[1,128]{1,0:T(1,128)} %bitcast.7, bf16[128,128]{1,0:T(8,128)(2,1)} %lgate_hbm.1, bf16[128,128]{1,0:T(8,128)(2,1)} %lvalue_hbm.1, bf16[128,128]{1,0:T(8,128)(2,1)} %rgate_hbm.1, ...), custom_call_target="tpu_custom_call" | custom-call | tf_op jit(solution)/shard_map/pallas_call | solution.py:513
  39.3 0.8 %copy.14 = bf16[64,26,128]{2,0,1:T(8,128)(2,1)} copy(bf16[64,26,128]{2,0,1:T(8,128)(2,1)S(1)} %bitcast.5) | data formatting | bytes 851968
